TPU v7x, 32 devices: a whole 2x2x4 slice. The times are simulated.
32 devices in a mesh: dp: 4 (over y, core), tensor: 8 (over z, x).
Axes of the slice: x: 2, y: 2, z: 4, core: 2. Of those that a mesh axis runs over, the one named last changes fastest.
Arguments:
- tokens: bfloat16 [512, 1024], P('dp', 'tensor'), may hold values from -6 to 6
- init_noise: float32 [512, 1024], P('dp', 'tensor'), may hold values from -1 to 1
- segment_ids: int32 [512], P('dp'), may hold values from 0 to 7, never falling along the last dimension, each value on 1 to 256 neighbouring positions
- target: float32 [512, 1024], P('dp', 'tensor'), may hold values from -6 to 6
- norm_gain: float32 [1024], replicated, may hold values from 0.1 to 1.9
- weight_in: bfloat16 [1024, 32768], P(None, 'tensor'), may hold values from -0.1875 to 0.1875
- weight_out: bfloat16 [32768, 1024], P('tensor'), may hold values from -0.03125 to 0.03125
- moment_in: float32 [1024, 32768], P('dp', 'tensor'), may hold values from -1.5 to 1.5
- moment_out: float32 [32768, 1024], P('tensor', 'dp'), may hold values from -1.5 to 1.5
Outputs:
- new_weight_in: bfloat16 [1024, 32768], P('dp', 'tensor')
- new_weight_out: bfloat16 [32768, 1024], P('tensor', 'dp')
- new_moment_in: float32 [1024, 32768], P('dp', 'tensor')
- new_moment_out: float32 [32768, 1024], P('tensor', 'dp')
- perturbation: float32 [512, 1024], P('dp', 'tensor')
Inputs may be any that keep to these rules, and one draw needn't show every extreme that they name: `segment_ids`: example ids never fall along the tokens; every example holds 1 to 256 tokens.
All inputs are finite; a program needn't handle non-finite values.
Results may differ from a plain program's by a relative error of at most 0.0051.
Values may be sent and summed in bfloat16 or wider, within the bound.
A program may use at most 128 MiB of HBM per device.

v0:
```python
import jax
import jax.numpy as jnp
from jax import lax
from jax.sharding import PartitionSpec as P

D = 1024
ASCENTS = 2


coeff = 0.7978845608
adv_init = 0.5
adv_step = 0.5
decay = 0.9
learn_rate = 0.01


def gelu_value(values):
    tangent = jnp.tanh(coeff * (values + 0.044715 * values * values * values))
    return 0.5 * values * (1.0 + tangent)


def gelu_slope(values):
    tangent = jnp.tanh(coeff * (values + 0.044715 * values * values * values))
    return 0.5 * (1.0 + tangent) + 0.5 * values * (1.0 - tangent * tangent) * coeff * (
        1.0 + 3.0 * 0.044715 * values * values
    )


def shards(
    tokens, init_noise, segment_ids, target, norm_gain, weight_in, weight_out, moment_in, moment_out
):
    dp_count = lax.axis_size("dp")
    local_tokens = tokens.shape[0]
    width_local = tokens.shape[1]
    loss_scale = (local_tokens * dp_count) ** (-0.5)
    column = lax.axis_index("tensor")
    labels = jnp.arange(2 * dp_count, dtype=jnp.int32)
    onehot = (segment_ids[:, None] == labels[None, :]).astype(jnp.float32)
    counts = lax.psum(jnp.sum(onehot, axis=0), "dp")
    perturb = adv_init * init_noise
    local_in = jnp.zeros(weight_in.shape, jnp.float32)
    local_out = jnp.zeros(weight_out.shape, jnp.float32)
    for ascent in range(ASCENTS):
        embedded = tokens.astype(jnp.float32) + perturb
        emb_bf = lax.optimization_barrier(embedded.astype(jnp.bfloat16))
        emb_local = emb_bf.astype(jnp.float32)
        gathered = lax.all_gather(emb_bf, "tensor", axis=1, tiled=True).astype(jnp.float32)
        inv_rms = lax.rsqrt(jnp.mean(gathered * gathered, axis=1, keepdims=True) + 1e-06)
        normed = (gathered * inv_rms * norm_gain).astype(jnp.bfloat16)
        preact = jnp.dot(normed, weight_in, preferred_element_type=jnp.float32)
        hidden = gelu_value(preact).astype(jnp.bfloat16)
        partial_value = jnp.dot(hidden, weight_out, preferred_element_type=jnp.float32)
        mixed = lax.psum_scatter(partial_value, "tensor", scatter_dimension=1, tiled=True)
        out_grad = (embedded + mixed - target) * loss_scale
        grad_whole = lax.all_gather(out_grad.astype(jnp.bfloat16), "tensor", axis=1, tiled=True)
        hidden_grad = (
            jnp.dot(grad_whole, weight_out.T, preferred_element_type=jnp.float32)
            * gelu_slope(preact)
        ).astype(jnp.bfloat16)
        part_in = jnp.dot(normed.T, hidden_grad, preferred_element_type=jnp.float32)
        part_out = jnp.dot(hidden.T, grad_whole, preferred_element_type=jnp.float32)
        local_in = local_in + part_in
        local_out = local_out + part_out
        if ascent + 1 < ASCENTS:
            normed_partial = jnp.dot(hidden_grad, weight_in.T, preferred_element_type=jnp.float32)
            normed_full = lax.psum(normed_partial, "tensor")
            scaled_full = normed_full * norm_gain
            row_dot = jnp.sum(scaled_full * gathered, axis=1, keepdims=True)
            scaled = lax.dynamic_slice_in_dim(scaled_full, column * width_local, width_local, 1)
            delta_grad = (
                out_grad + inv_rms * scaled - emb_local * inv_rms * inv_rms * inv_rms * row_dot / D
            )
            row_squares = jnp.sum(delta_grad * delta_grad, axis=1)
            square_sums = lax.psum(jnp.sum(onehot * row_squares[:, None], axis=0), ("dp", "tensor"))
            root_mean = jnp.sqrt(square_sums / (counts * D) + 1e-06)
            token_scale = jnp.sum(onehot * (adv_step / root_mean)[None, :], axis=1)
            perturb = perturb + delta_grad * token_scale[:, None]
    summed_in, summed_out = (
        lax.psum_scatter(local_in, "dp", scatter_dimension=0, tiled=True),
        lax.psum_scatter(local_out, "dp", scatter_dimension=1, tiled=True),
    )
    dp_rows = moment_in.shape[0]
    offset = lax.axis_index("dp") * dp_rows
    own_in = lax.dynamic_slice_in_dim(weight_in, offset, dp_rows, 0)
    own_out = lax.dynamic_slice_in_dim(weight_out, offset, dp_rows, 1)
    new_moment_in = decay * moment_in + summed_in / ASCENTS
    new_moment_out = decay * moment_out + summed_out / ASCENTS
    new_weight_in = (own_in.astype(jnp.float32) - learn_rate * new_moment_in).astype(jnp.bfloat16)
    new_weight_out = (own_out.astype(jnp.float32) - learn_rate * new_moment_out).astype(
        jnp.bfloat16
    )
    return (new_weight_in, new_weight_out, new_moment_in, new_moment_out, perturb)


def solution(mesh):
    placed = (
        P("dp", "tensor"),
        P("dp", "tensor"),
        P("dp"),
        P("dp", "tensor"),
        P(),
        P(None, "tensor"),
        P("tensor", None),
        P("dp", "tensor"),
        P("tensor", "dp"),
    )
    return jax.shard_map(
        shards,
        mesh=mesh,
        in_specs=placed,
        out_specs=(
            P("dp", "tensor"),
            P("tensor", "dp"),
            P("dp", "tensor"),
            P("tensor", "dp"),
            P("dp", "tensor"),
        ),
        check_vma=False,
    )
```

profile of v0, /device:TPU:1, one launch (start us, length us, event | category | flops | bytes accessed | tf_op | source)
XLA Modules:
  0.0 668.6 jit_solution(5193711756764205640)
XLA Ops:
  7.2 0.9 fusion.27
  8.1 23.5 %all_gather.12 = bf16[128,1024]{1,0:T(8,128)(2,1)S(1)} all-gather(bf16[128,128]{1,0:T(8,128)(2,1)S(1)} %fusion.27), channel_id=1, replica_groups=mesh['dp'=4,'tensor'=8] {'tensor'}, dimensions={1}, use_global_device_ids=true | all-gather | bytes 294912 | tf_op jit(solution)/shard_map/all_gather | solution.py:47
  31.7 4.9 fusion.21
  36.6 0.9 slice-done.3
  37.5 2.4 fusion.29
  40.0 65.0 %reduce-scatter.5.cloned.1.call-done = f32[128,128]{1,0:T(8,128)} async-done(((f32[128,1024]{1,0:T(8,128)}), f32[128,128]{1,0:T(8,128)}) %reduce-scatter.5.cloned.1.call-update) | async-done | bytes 65552 | tf_op jit(solution)/shard_map/reduce_scatter | solution.py:53
  105.0 1.0 fusion.31
  106.0 22.5 %all_gather.13 = bf16[128,1024]{1,0:T(8,128)(2,1)S(1)} all-gather(bf16[128,128]{1,0:T(8,128)(2,1)S(1)} %get-tuple-element.17), channel_id=1, replica_groups=mesh['dp'=4,'tensor'=8] {'tensor'}, dimensions={1}, use_global_device_ids=true | all-gather | bytes 294912 | tf_op jit(solution)/shard_map/all_gather | solution.py:55
  128.5 7.0 %fusion = bf16[128,4096]{1,0:T(8,128)(2,1)S(1)} fusion(bf16[128,1024]{1,0:T(8,128)(2,1)S(1)} %all_gather.13, bf16[4096,1024]{1,0:T(8,128)(2,1)} %param.15, f32[128,4096]{1,0:T(8,128)S(1)} %fusion.21), kind=kOutput, calls=%fused_computation.4 | convolution fusion | flops 1083703296 | bytes 11796480 | tf_op jit(solution)/shard_map/dot_general | solution.py:57
  135.6 1.0 copy-done.1
  136.5 3.7 fusion.32
  140.3 74.7 %all-reduce.2.cloned.1.call-done = f32[128,1024]{1,0:T(8,128)} async-done(((f32[128,1024]{1,0:T(8,128)}), f32[128,1024]{1,0:T(8,128)}) %all-reduce.2.cloned.1.call-update) | async-done | bytes 524304 | tf_op jit(solution)/shard_map/psum | solution.py:66
  215.0 1.2 fusion.18
  216.2 0.2 multiply_reduce_fusion
  216.5 7.4 %psum.23 = f32[8]{0:T(128)S(1)} all-reduce(f32[8]{0:T(128)S(1)} %get-tuple-element.5), channel_id=1, replica_groups=mesh['dp'=4,'tensor'=8] {'dp'}, use_global_device_ids=true, to_apply=%region_8.0 | all-reduce | flops 8 | bytes 64 | tf_op jit(solution)/shard_map/psum | solution.py:39
  224.0 38.9 %psum.22 = f32[8]{0:T(128)S(1)} all-reduce(f32[8]{0:T(128)S(1)} %get-tuple-element.6), channel_id=1, replica_groups=mesh['dp'=4,'tensor'=8] {'dp','tensor'}, use_global_device_ids=true, to_apply=%region_6.0 | all-reduce | flops 8 | bytes 64 | tf_op jit(solution)/shard_map/psum | solution.py:74
  263.0 22.0 %all_gather.14 = bf16[128,1024]{1,0:T(8,128)(2,1)S(1)} all-gather(bf16[128,128]{1,0:T(8,128)(2,1)S(1)} %get-tuple-element.11), channel_id=1, replica_groups=mesh['dp'=4,'tensor'=8] {'tensor'}, dimensions={1}, use_global_device_ids=true | all-gather | bytes 294912 | tf_op jit(solution)/shard_map/all_gather | solution.py:47
  285.2 4.7 fusion.24
  289.9 5.7 fusion.30
  295.7 9.7 %fusion.28 = f32[4096,1024]{1,0:T(8,128)} fusion(bf16[128,1024]{1,0:T(8,128)(2,1)S(1)} %all_gather.13, f32[128,4096]{1,0:T(8,128)} %copy-done), kind=kOutput, calls=%fused_computation.59 | convolution fusion | flops 1078460416 | bytes 19136512 | tf_op jit(solution)/shard_map/dot_general | solution.py:61
  305.4 55.5 %reduce-scatter.7.cloned.1.call-done = f32[128,128]{1,0:T(8,128)} async-done(((f32[128,1024]{1,0:T(8,128)}), f32[128,128]{1,0:T(8,128)}) %reduce-scatter.7.cloned.1.call-update) | async-done | bytes 65552 | tf_op jit(solution)/shard_map/reduce_scatter | solution.py:53
  360.8 0.9 multiply_convert_fusion.2
  361.7 22.4 %all_gather.15 = bf16[128,1024]{1,0:T(8,128)(2,1)S(1)} all-gather(bf16[128,128]{1,0:T(8,128)(2,1)S(1)} %multiply_convert_fusion.2), channel_id=1, replica_groups=mesh['dp'=4,'tensor'=8] {'tensor'}, dimensions={1}, use_global_device_ids=true | all-gather | bytes 294912 | tf_op jit(solution)/shard_map/all_gather | solution.py:55
  384.1 13.9 %convolution_add_fusion = f32[4096,1024]{1,0:T(8,128)} fusion(f32[4096,1024]{1,0:T(8,128)} %fusion.28, bf16[128,1024]{1,0:T(8,128)(2,1)S(1)} %all_gather.15, f32[128,4096]{1,0:T(8,128)S(1)} %fusion.24), kind=kOutput, calls=%fused_computation | convolution fusion | flops 1082654720 | bytes 35913728 | tf_op jit(solution)/shard_map/dot_general | solution.py:61
  398.0 0.3 reduce-scatter.9.cloned.1.call-start
  398.3 3.7 fusion.19
  402.0 7.8 %fusion.1 = bf16[128,4096]{1,0:T(8,128)(2,1)} fusion(bf16[128,1024]{1,0:T(8,128)(2,1)S(1)} %all_gather.15, bf16[4096,1024]{1,0:T(8,128)(2,1)} %param.15, f32[128,4096]{1,0:T(8,128)S(1)} %fusion.24), kind=kOutput, calls=%fused_computation.5 | convolution fusion | flops 1083703296 | bytes 11796480 | tf_op jit(solution)/shard_map/dot_general | solution.py:57
  409.8 14.5 %convolution_add_fusion.1 = f32[1024,4096]{1,0:T(8,128)} fusion(f32[1024,4096]{1,0:T(8,128)S(1)} %fusion.19, bf16[128,4096]{1,0:T(8,128)(2,1)} %fusion.1, bf16[128,1024]{1,0:T(8,128)(2,1)S(1)} %all_gather.14, f32[128]{0:T(128)S(1)} %add_rsqrt_fusion, f32[1024]{0:T(1024)S(1)} %copy-done.2), kind=kOutput, calls=%fused_computation.1 | convolution fusion | flops 1078460416 | bytes 34869760 | tf_op jit(solution)/shard_map/dot_general | solution.py:60
  424.4 102.0 %reduce-scatter.11.cloned.1.call-done = f32[4096,256]{1,0:T(8,128)} async-done(((f32[4096,1024]{1,0:T(8,128)}), f32[4096,256]{1,0:T(8,128)}) %reduce-scatter.11.cloned.1.call-update) | async-done | bytes 4194320 | tf_op jit(solution)/shard_map/reduce_scatter | solution.py:80
  526.4 7.7 %subtract_convert_fusion = (bf16[4096,256]{1,0:T(8,128)(2,1)}, f32[4096,256]{1,0:T(8,128)}) fusion(bf16[4096,1024]{1,0:T(8,128)(2,1)} %param.15, s32[]{:T(128)S(6)} %select_n.7, f32[4096,256]{1,0:T(8,128)} %reduce-scatter.11.cloned.1.call-done, f32[4096,256]{1,0:T(8,128)} %param.17), kind=kLoop, calls=%fused_computation.6 | loop fusion | flops 7340032 | bytes 16777220 | tf_op jit(solution)/shard_map/convert_element_type | solution.py:89
  534.1 119.8 %reduce-scatter.9.cloned.1.call-done = f32[256,4096]{1,0:T(8,128)} async-done(((f32[1024,4096]{1,0:T(8,128)}), f32[256,4096]{1,0:T(8,128)}) %reduce-scatter.9.cloned.1.call-update) | async-done | bytes 4194320 | tf_op jit(solution)/shard_map/reduce_scatter | solution.py:79
  653.9 8.2 %subtract_convert_fusion.1 = (bf16[256,4096]{1,0:T(8,128)(2,1)}, f32[256,4096]{1,0:T(8,128)}) fusion(bf16[1024,4096]{1,0:T(8,128)(2,1)} %param.14, s32[]{:T(128)S(6)} %select_n.7, f32[256,4096]{1,0:T(8,128)} %reduce-scatter.9.cloned.1.call-done, f32[256,4096]{1,0:T(8,128)} %param.16), kind=kLoop, calls=%fused_computation.8 | loop fusion | flops 7340032 | bytes 16777220 | tf_op jit(solution)/shard_map/convert_element_type | solution.py:88
  (41 shorter events, 0.9 us)
Async XLA Ops:
  7.2 97.8 %reduce-scatter.5.cloned.1.call-start = ((), (), s32[]{:S(2)}) async-start(), calls=%async_computation.4 | async-start | bytes 589824 | tf_op jit(solution)/shard_map/reduce_scatter | solution.py:53
  31.6 5.0 slice-start.2
  31.7 5.8 slice-start.3
  37.5 91.0 %copy-start = (f32[128,4096]{1,0:T(8,128)}, f32[128,4096]{1,0:T(8,128)S(1)}, u32[]{:S(2)}) copy-start(f32[128,4096]{1,0:T(8,128)S(1)} %fusion.21) | copy-start | bytes 6291460
  37.5 67.5 %copy-start.3 = (f32[128,128]{1,0:T(8,128)S(1)}, f32[128,128]{1,0:T(8,128)}, u32[]{:S(2)}) copy-start(f32[128,128]{1,0:T(8,128)} %param.10) | copy-start | bytes 196612
  37.5 67.5 %copy-start.4 = (bf16[128,128]{1,0:T(8,128)(2,1)S(1)}, bf16[128,128]{1,0:T(8,128)(2,1)}, u32[]{:S(2)}) copy-start(bf16[128,128]{1,0:T(8,128)(2,1)} %param.9) | copy-start | bytes 98308
  37.5 67.5 %copy-start.5 = (f32[128,128]{1,0:T(8,128)S(1)}, f32[128,128]{1,0:T(8,128)}, u32[]{:S(2)}) copy-start(f32[128,128]{1,0:T(8,128)} %param.12) | copy-start | bytes 196612
  40.0 175.1 %all-reduce.2.cloned.1.call-start = ((), (), s32[]{:S(2)}) async-start(), calls=%async_computation.5 | async-start | bytes 1048576 | tf_op jit(solution)/shard_map/psum | solution.py:66
  105.0 31.5 %slice-start = ((s8[8388608]{0:T(1024)(128)(4,1)}), s8[4194304]{0:T(1024)(128)(4,1)S(1)}, s32[]{:S(2)}) async-start(s8[8388608]{0:T(1024)(128)(4,1)} %bitcast.14), calls=%async_computation.9 | async-start | bytes 8388608
  128.5 8.0 %slice-start.1 = ((s8[8388608]{0:T(1024)(128)(4,1)}), s8[4194304]{0:T(1024)(128)(4,1)S(1)}, s32[]{:S(2)}) async-start(s8[8388608]{0:T(1024)(128)(4,1)} %bitcast.14), calls=%async_computation.10 | async-start | bytes 8388608
  135.5 1.0 copy-start.1
  136.5 78.5 %copy-start.2 = (f32[1024]{0:T(1024)S(1)}, f32[1024]{0:T(1024)}, u32[]{:S(2)}) copy-start(f32[1024]{0:T(1024)} %param.13) | copy-start | bytes 12292
  136.5 79.9 %copy-start.7 = (s32[128]{0:T(128)S(1)}, s32[128]{0:T(128)}, u32[]{:S(2)}) copy-start(s32[128]{0:T(128)} %param.11) | copy-start | bytes 1540
  140.2 220.6 %reduce-scatter.7.cloned.1.call-start = ((), (), s32[]{:S(2)}) async-start(), calls=%async_computation.6 | async-start | bytes 589824 | tf_op jit(solution)/shard_map/reduce_scatter | solution.py:53
  263.0 97.8 %copy-start.6 = (f32[128,128]{1,0:T(8,128)}, f32[128,128]{1,0:T(8,128)S(1)}, u32[]{:S(2)}) copy-start(f32[128,128]{1,0:T(8,128)S(1)} %get-tuple-element.12) | copy-start | bytes 196612
  295.6 230.8 %reduce-scatter.11.cloned.1.call-start = ((), (), s32[]{:S(2)}) async-start(), calls=%async_computation.8 | async-start | bytes 20971520 | tf_op jit(solution)/shard_map/reduce_scatter | solution.py:80
  398.0 255.9 %reduce-scatter.9.cloned.1.call-start = ((), (), s32[]{:S(2)}) async-start(), calls=%async_computation.7 | async-start | bytes 20971520 | tf_op jit(solution)/shard_map/reduce_scatter | solution.py:79
Sparse Core Ops, SparseCore 0:
  40.1 64.8 reduce-scatter.4
  140.4 74.6 all-reduce.1
  295.7 65.0 reduce-scatter.6
  398.2 128.1 reduce-scatter.10
  528.8 125.0 reduce-scatter.8
where the time goes:
time: 670 us; the launch traced here: 669 us
  waiting for transfers between devices  417 us (62%)
  blocking collectives  137 us (20%)
  matrix products  78 us (12%)
  other arithmetic  20.7 us (3%)
  between operations  13.9 us (2%)
    reduce_scatter x2, waiting for transfers between devices, shards(): lax.psum_scatter(partial_value, 'tensor', scatter_dimension=1, tiled=True)  120 us
    reduce_scatter x1, waiting for transfers between devices, shards(): lax.psum_scatter(local_in, 'dp', scatter_dimension=0, tiled=True)  120 us
    reduce_scatter x1, waiting for transfers between devices, shards(): lax.psum_scatter(local_out, 'dp', scatter_dimension=1, tiled=True)  102 us
    psum x1, waiting for transfers between devices, shards(): normed_full = lax.psum(normed_partial, 'tensor')  74.7 us
    all_gather x2, blocking collectives, shards(): lax.all_gather(emb_bf, 'tensor', axis=1, tiled=True).astype(jnp.float32)  45.5 us
    all_gather x2, blocking collectives, shards(): lax.all_gather(out_grad.astype(jnp.bfloat16), 'tensor', axis=1, tiled=True)  44.9 us
    psum x1, blocking collectives, shards(): lax.psum(jnp.sum(onehot * row_squares[:, None], axis=0), ('dp', 'tensor'))  38.9 us
    dot_general x2, matrix products, shards(): part_out = jnp.dot(hidden.T, grad_whole, preferred_element_type=jnp.float32)  23.6 us
  transfers between devices with their start and end apart: 5, of which 5 were waited for; matrix products, arithmetic and copies ran while one was open for 7% of the time, Pallas kernels for 0%

commit v1 on v0

v1 whole, which is shorter than its diff:
```python
import functools

import jax
import jax.numpy as jnp
from jax import lax
from jax.experimental import pallas as pl
from jax.experimental.pallas import tpu as pltpu
from jax.sharding import PartitionSpec as P

ASCENTS = 2

coeff = 0.7978845608
adv_init = 0.5
adv_step = 0.5
decay = 0.9
learn_rate = 0.01


def gelu_both(values):
    square = values * values
    tangent = jnp.tanh(coeff * (values + 0.044715 * square * values))
    half = 0.5 * (1.0 + tangent)
    slope = half + 0.5 * values * (1.0 - tangent * tangent) * coeff * (1.0 + 3.0 * 0.044715 * square)
    return values * half, slope


class Place:
    def __init__(self):
        self.dp_count, self.tensor_count = lax.axis_size("dp"), lax.axis_size("tensor")
        self.ys, self.zs = self.dp_count // 2, self.tensor_count // 2
        self.dp, self.tensor = lax.axis_index("dp"), lax.axis_index("tensor")
        self.y, self.core = self.dp // 2, self.dp % 2
        self.z, self.x = self.tensor // 2, self.tensor % 2


def enter(at):
    barrier = pltpu.get_barrier_semaphore()
    for step in range(1, at.tensor_count):
        there = (at.dp, lax.rem(at.tensor + step, at.tensor_count))
        pl.semaphore_signal(barrier, inc=1, device_id=there, device_id_type=pl.DeviceIdType.MESH)
    for step in range(1, at.dp_count):
        there = (lax.rem(at.dp + step, at.dp_count), at.tensor)
        pl.semaphore_signal(barrier, inc=1, device_id=there, device_id_type=pl.DeviceIdType.MESH)
    pl.semaphore_wait(barrier, at.tensor_count + at.dp_count - 2)


def send(source, target, sems, number, there):
    copy = pltpu.make_async_remote_copy(
        src_ref=source,
        dst_ref=target,
        send_sem=sems[0].at[number],
        recv_sem=sems[1].at[number],
        device_id=there,
        device_id_type=pl.DeviceIdType.MESH,
    )
    copy.start()
    return copy


def gather_copies(dp_count, tensor_count):
    zs, ys = tensor_count // 2, dp_count // 2
    return (zs - 1) + zs + 2 * zs * (ys - 1) + 2 * zs * ys


def gather(at, own_ref, whole_ref, sems):
    rows, cols = own_ref.shape
    numbers = iter(range(gather_copies(at.dp_count, at.tensor_count)))
    started, to_core = [], []

    def place(dp, tensor):
        span = pl.ds(pl.multiple_of(dp * rows, rows), rows)
        if len(whole_ref.shape) == 3:
            return (tensor, span)
        return (span, pl.ds(pl.multiple_of(tensor * cols, cols), cols))

    def block(dp, tensor):
        return whole_ref.at[place(dp, tensor)]

    def start(source, dp, tensor, there):
        copy = send(source, block(dp, tensor), sems, next(numbers), there)
        started.append(copy)
        return copy

    def share(source, dp, tensor):
        to_core.append(start(source, dp, tensor, (at.y * 2 + 1 - at.core, at.tensor)))

    other_x = (at.dp, at.z * 2 + 1 - at.x)
    along_z = {
        k: start(
            own_ref, at.dp, at.tensor, (at.dp, lax.rem(at.z + at.zs - k, at.zs) * 2 + at.x)
        )
        for k in range(1, at.zs)
    }
    whole_ref[place(at.dp, at.tensor)] = own_ref[...]
    along_x, along_y, corner = {}, {}, {}
    column = [lax.rem(at.z + k, at.zs) * 2 for k in range(at.zs)]
    line = [lax.rem(at.y + j, at.ys) * 2 + at.core for j in range(at.ys)]
    back = [lax.rem(at.y + at.ys - j, at.ys) * 2 + at.core for j in range(at.ys)]
    for k in range(at.zs):
        mine = column[k] + at.x
        source = own_ref
        if k:
            along_z[k].wait_recv()
            source = block(at.dp, mine)
        along_x[k] = start(source, at.dp, mine, other_x)
        for j in range(1, at.ys):
            along_y[k, j] = start(source, at.dp, mine, (back[j], at.tensor))
        share(source, at.dp, mine)
    for k in range(at.zs):
        mine, beside = column[k] + at.x, column[k] + 1 - at.x
        along_x[k].wait_recv()
        for j in range(1, at.ys):
            if k % 2 == 0:
                corner[k, j] = start(
                    block(at.dp, beside), at.dp, beside, (back[j], at.tensor)
                )
        share(block(at.dp, beside), at.dp, beside)
        for j in range(1, at.ys):
            along_y[k, j].wait_recv()
            if k % 2 == 1:
                corner[k, j] = start(block(line[j], mine), line[j], mine, other_x)
            share(block(line[j], mine), line[j], mine)
    for k in range(at.zs):
        beside = column[k] + 1 - at.x
        for j in range(1, at.ys):
            corner[k, j].wait_recv()
            share(block(line[j], beside), line[j], beside)
    for copy in to_core:
        copy.wait_recv()
    for copy in started:
        copy.wait_send()


def scatter_sum(at, partial_ref, landing, sems):
    cols = landing.shape[2]

    def own(tensor):
        if len(partial_ref.shape) == 3:
            return (tensor,)
        return (slice(None), pl.ds(pl.multiple_of(tensor * cols, cols), cols))

    copies = []
    for step in range(1, at.tensor_count):
        there = lax.rem(at.tensor + step, at.tensor_count)
        copies.append(
            send(
                partial_ref.at[own(there)], landing.at[step - 1], sems, step - 1, (at.dp, there)
            )
        )
    value = partial_ref[own(at.tensor)].astype(jnp.float32)
    for step, copy in enumerate(copies):
        copy.wait_recv()
        value = value + landing[step].astype(jnp.float32)
    for copy in copies:
        copy.wait_send()
    return value


def first_kernel(emb_ref, whole_ref, *sems):
    at = Place()
    enter(at)
    gather(at, emb_ref, whole_ref, sems)


def forward_kernel(
    partial_ref, tokens_ref, perturb_ref, target_ref, whole_ref, out_grad_ref,
    landing, own, send_sum, recv_sum, send_all, recv_all, *, scale,
):
    at = Place()
    enter(at)
    mixed = scatter_sum(at, partial_ref, landing, (send_sum, recv_sum))
    embedded = tokens_ref[...].astype(jnp.float32) + perturb_ref[...]
    out_grad = (embedded + mixed - target_ref[...]) * scale
    own[...] = out_grad.astype(jnp.bfloat16)
    out_grad_ref[...] = out_grad
    gather(at, own, whole_ref, (send_all, recv_all))


def ascent_kernel(
    partial_ref, tokens_ref, perturb_ref, out_grad_ref, inv_ref, gain_ref, ids_ref,
    whole_ref, new_ref,
    landing, own, stats, stats_in, squares, squares_in,
    send_sum, recv_sum, send_stat, recv_stat, send_square, recv_square, send_all, recv_all,
    *, features,
):
    at = Place()
    enter(at)
    rows = own.shape[0]
    examples = squares.shape[0] // 2
    scaled = gain_ref[...] * scatter_sum(at, partial_ref, landing, (send_sum, recv_sum))
    tokens = tokens_ref[...].astype(jnp.float32)
    perturb = perturb_ref[...]
    emb = (tokens + perturb).astype(jnp.bfloat16).astype(jnp.float32)
    inv = inv_ref[...]
    base = out_grad_ref[...] + inv * scaled
    radial = emb * (inv * inv * inv * (1.0 / features))
    lane = lax.broadcasted_iota(jnp.int32, (rows, rows), 1)
    table = jnp.where(lane == 0, jnp.sum(scaled * emb, axis=1, keepdims=True), 0.0)
    table = jnp.where(lane == 1, jnp.sum(base * base, axis=1, keepdims=True), table)
    table = jnp.where(lane == 2, jnp.sum(base * radial, axis=1, keepdims=True), table)
    table = jnp.where(lane == 3, jnp.sum(radial * radial, axis=1, keepdims=True), table)
    own_stats = table.T[:8, :]
    stats[...] = own_stats
    copies = [
        send(
            stats, stats_in.at[step - 1], (send_stat, recv_stat), step - 1,
            (at.dp, lax.rem(at.tensor + step, at.tensor_count)),
        )
        for step in range(1, at.tensor_count)
    ]
    summed = own_stats
    for step, copy in enumerate(copies):
        copy.wait_recv()
        summed = summed + stats_in[step]
    for copy in copies:
        copy.wait_send()
    row_dot = summed[0:1, :]
    row_squares = (
        summed[1:2, :] - 2.0 * row_dot * summed[2:3, :] + row_dot * row_dot * summed[3:4, :]
    )
    label = lax.broadcasted_iota(jnp.int32, (examples, rows), 0)
    onehot = (label == ids_ref[...]).astype(jnp.float32)
    local = jnp.concatenate(
        [
            jnp.broadcast_to(
                jnp.sum(onehot * row_squares, axis=1, keepdims=True), (examples, rows)
            ),
            jnp.broadcast_to(jnp.sum(onehot, axis=1, keepdims=True), (examples, rows)),
        ],
        axis=0,
    )
    squares[...] = local
    copies = [
        send(
            squares, squares_in.at[step - 1], (send_square, recv_square), step - 1,
            (lax.rem(at.dp + step, at.dp_count), at.tensor),
        )
        for step in range(1, at.dp_count)
    ]
    for step, copy in enumerate(copies):
        copy.wait_recv()
        local = local + squares_in[step]
    for copy in copies:
        copy.wait_send()
    square_sums, counts = jnp.maximum(local[:examples], 0.0), local[examples:]
    root_mean = jnp.sqrt(square_sums / (jnp.maximum(counts, 1.0) * features) + 1e-06)
    token_scale = jnp.sum(onehot * (adv_step / root_mean), axis=0, keepdims=True)
    high = lax.broadcasted_iota(jnp.int32, (rows, rows), 0)
    columns = jnp.where(high == 0, token_scale, jnp.where(high == 1, row_dot, 0.0)).T
    perturb = perturb + (base - radial * columns[:, 1:2]) * columns[:, 0:1]
    new_ref[...] = perturb
    own[...] = (tokens + perturb).astype(jnp.bfloat16)
    gather(at, own, whole_ref, (send_all, recv_all))


def talk(kernel, number, out_shape, scratch, *args):
    vmem = pl.BlockSpec(memory_space=pltpu.VMEM)
    return pl.pallas_call(
        kernel,
        name=f"talk{number}",
        out_shape=out_shape,
        in_specs=[vmem] * len(args),
        out_specs=jax.tree.map(lambda _: vmem, out_shape),
        scratch_shapes=scratch,
        compiler_params=pltpu.CompilerParams(collective_id=number, has_side_effects=True),
    )(*args)


def shards(
    tokens, init_noise, segment_ids, target, norm_gain, weight_in, weight_out, moment_in, moment_out
):
    dp_count, tensor_count = lax.axis_size("dp"), lax.axis_size("tensor")
    rows, width = tokens.shape
    features = weight_in.shape[0]
    loss_scale = (rows * dp_count) ** (-0.5)
    me = lax.axis_index("dp")
    own_rows = moment_in.shape[0]
    examples = 2 * dp_count
    gain_own = lax.dynamic_slice_in_dim(norm_gain, lax.axis_index("tensor") * width, width, 0)
    dma = pltpu.SemaphoreType.DMA
    copies = gather_copies(dp_count, tensor_count)
    gather_sems = [dma((copies,)), dma((copies,))]
    sum_sems = [dma((tensor_count - 1,)), dma((tensor_count - 1,))]
    square_sems = [dma((dp_count - 1,)), dma((dp_count - 1,))]
    landing = pltpu.VMEM((tensor_count - 1, rows, width), jnp.bfloat16)
    own_block = pltpu.VMEM((rows, width), jnp.bfloat16)
    narrow = width % 128 != 0
    total = rows * dp_count
    whole = jax.ShapeDtypeStruct(
        (tensor_count, total, width) if narrow else (total, features), jnp.bfloat16
    )

    def flat(array):
        return array.transpose(1, 0, 2).reshape(total, features) if narrow else array

    def split(array):
        return array.reshape(rows, tensor_count, width).transpose(1, 0, 2) if narrow else array

    block = jax.ShapeDtypeStruct((rows, width), jnp.float32)
    perturb = adv_init * init_noise
    emb_bf = (tokens.astype(jnp.float32) + perturb).astype(jnp.bfloat16)
    gathered_bf = talk(first_kernel, 0, whole, gather_sems, emb_bf)
    grad_in = jnp.zeros(moment_in.shape, jnp.float32)
    grad_out = jnp.zeros(moment_out.shape, jnp.float32)
    for ascent in range(ASCENTS):
        gathered = flat(gathered_bf).astype(jnp.float32)
        inv_rms = lax.rsqrt(jnp.mean(gathered * gathered, axis=1, keepdims=True) + 1e-06)
        normed = (gathered * inv_rms * norm_gain).astype(jnp.bfloat16)
        preact = jnp.dot(normed, weight_in, preferred_element_type=jnp.float32)
        hidden, slope = gelu_both(preact)
        hidden = hidden.astype(jnp.bfloat16)
        hidden_own = lax.dynamic_slice_in_dim(hidden, me * rows, rows, 0)
        partial_value = jnp.dot(
            hidden_own, weight_out, preferred_element_type=jnp.float32
        ).astype(jnp.bfloat16)
        grad_whole, out_grad = talk(
            functools.partial(forward_kernel, scale=loss_scale), 1 + 2 * ascent, (whole, block),
            [landing, own_block, *sum_sems, *gather_sems],
            split(partial_value), tokens, perturb, target,
        )
        grad_whole = flat(grad_whole)
        hidden_grad = (
            jnp.dot(grad_whole, weight_out.T, preferred_element_type=jnp.float32) * slope
        ).astype(jnp.bfloat16)
        if ascent + 1 < ASCENTS:
            hidden_grad_own = lax.dynamic_slice_in_dim(hidden_grad, me * rows, rows, 0)
            normed_partial = jnp.dot(
                hidden_grad_own, weight_in.T, preferred_element_type=jnp.float32
            ).astype(jnp.bfloat16)
            inv_own = lax.dynamic_slice_in_dim(inv_rms, me * rows, rows, 0)
            small = pltpu.VMEM((8, rows), jnp.float32)
            gathered_bf, perturb = talk(
                functools.partial(ascent_kernel, features=features), 2 + 2 * ascent,
                (whole, block),
                [
                    landing, own_block, small,
                    pltpu.VMEM((tensor_count - 1, 8, rows), jnp.float32),
                    pltpu.VMEM((2 * examples, rows), jnp.float32),
                    pltpu.VMEM((dp_count - 1, 2 * examples, rows), jnp.float32),
                    *sum_sems, *sum_sems, *square_sems, *gather_sems,
                ],
                split(normed_partial), tokens, perturb, out_grad, inv_own,
                gain_own.reshape(1, width), segment_ids.reshape(1, rows),
            )
        normed_cols = lax.dynamic_slice_in_dim(normed, me * own_rows, own_rows, 1)
        grad_cols = lax.dynamic_slice_in_dim(grad_whole, me * own_rows, own_rows, 1)
        grad_in = grad_in + jnp.dot(normed_cols.T, hidden_grad, preferred_element_type=jnp.float32)
        grad_out = grad_out + jnp.dot(hidden.T, grad_cols, preferred_element_type=jnp.float32)
    own_in = lax.dynamic_slice_in_dim(weight_in, me * own_rows, own_rows, 0)
    own_out = lax.dynamic_slice_in_dim(weight_out, me * own_rows, own_rows, 1)
    new_moment_in = decay * moment_in + grad_in / ASCENTS
    new_moment_out = decay * moment_out + grad_out / ASCENTS
    new_weight_in = (own_in.astype(jnp.float32) - learn_rate * new_moment_in).astype(jnp.bfloat16)
    new_weight_out = (own_out.astype(jnp.float32) - learn_rate * new_moment_out).astype(
        jnp.bfloat16
    )
    return (new_weight_in, new_weight_out, new_moment_in, new_moment_out, perturb)


def solution(mesh):
    placed = (
        P("dp", "tensor"),
        P("dp", "tensor"),
        P("dp"),
        P("dp", "tensor"),
        P(),
        P(None, "tensor"),
        P("tensor", None),
        P("dp", "tensor"),
        P("tensor", "dp"),
    )
    return jax.shard_map(
        shards,
        mesh=mesh,
        in_specs=placed,
        out_specs=(
            P("dp", "tensor"),
            P("tensor", "dp"),
            P("dp", "tensor"),
            P("tensor", "dp"),
            P("dp", "tensor"),
        ),
        check_vma=False,
    )
```

time: 670 us -> 204 us (0.30)
  waiting for transfers between devices: 417 us -> 0 us
  blocking collectives: 137 us -> 0 us
  Pallas kernels: 0 us -> 102 us
  between operations: 13.9 us -> 0.75 us
  other arithmetic: 20.7 us -> 7.72 us
  matrix products: 78 us -> 86.9 us
    reduce_scatter x4 -> x0, waiting for transfers between devices: 342 us -> none  [the longest x2 120 us: shards(): lax.psum_scatter(partial_value, 'tensor', scatter_dimension=1, tiled=True)]
    pallas_call x0 -> x4, Pallas kernels: none -> 102 us  [talk(): pl.pallas_call(kernel, name=f'talk{number}', out_shape=out_shape, in_spec...]
    all_gather x4 -> x0, blocking collectives: 90.4 us -> none  [the longest x2 45.5 us: shards(): lax.all_gather(emb_bf, 'tensor', axis=1, tiled=True).astype(jnp.float32)]
    psum x1 -> x0, waiting for transfers between devices: 74.7 us -> none  [shards(): normed_full = lax.psum(normed_partial, 'tensor')]
    psum x2 -> x0, blocking collectives: 46.3 us -> none  [the longest x1 38.9 us: shards(): lax.psum(jnp.sum(onehot * row_squares[:, None], axis=0), ('dp', 'tensor'))]
    convert_element_type x6 -> x2, other arithmetic: 18.8 us -> 3.21 us  [shards(): normed = (gathered * inv_rms * norm_gain).astype(jnp.bfloat16)]
    dot_general x2, matrix products: 9.57 us -> 23.5 us  [shards(): preact = jnp.dot(normed, weight_in, preferred_element_type=jnp.float32)]
    dot_general x2 -> x1, matrix products: 14.8 us -> 12.3 us  [shards(): jnp.dot(grad_whole, weight_out.T, preferred_element_type=jnp.float32)]
  transfers between devices with their start and end apart: 5 -> 0, of which waited for: 5 -> 0; matrix products, arithmetic and copies ran while one was open for 7% -> 0% of each run, Pallas kernels for 0% -> 0%
where the time goes in v1:
time: 204 us
  Pallas kernels  102 us (50%)
  matrix products  86.9 us (43%)
  other arithmetic  7.72 us (4%)
  local copies, waits for them, and re-layouts  6.69 us (3%)
    pallas_call x4, Pallas kernels, talk(): pl.pallas_call(kernel, name=f'talk{number}', out_shape=out_shape, in_spec...  102 us
    dot_general x2, matrix products, shards(): preact = jnp.dot(normed, weight_in, preferred_element_type=jnp.float32)  23.5 us
    dot_general x2, matrix products, shards(): jnp.dot(normed_cols.T, hidden_grad, preferred_element_type=jnp.float32)  22.8 us
    dot_general x2, matrix products, shards(): jnp.dot(hidden.T, grad_cols, preferred_element_type=jnp.float32)  14 us
    dot_general x1, matrix products, shards(): jnp.dot(grad_whole, weight_out.T, preferred_element_type=jnp.float32)  12.3 us
    dot_general x2, matrix products, shards(): jnp.dot(hidden_own, weight_out, preferred_element_type=jnp.float32)  7.37 us
    dot_general x1, matrix products, shards(): jnp.dot(hidden_grad_own, weight_in.T, preferred_element_type=jnp.float32)  6.99 us
    unnamed x15, local copies, waits for them, and re-layouts  4.59 us

profile of v1, /device:TPU:1, one launch (start us, length us, event | category | flops | bytes accessed | tf_op | source)
XLA Modules:
  0.0 203.9 jit_solution(7017409760090788228)
XLA Ops:
  0.6 1.3 dynamic-slice_bitcast_fusion.gain_ref
  1.9 1.5 broadcast_multiply_fusion
  3.4 19.2 %talk0.1 = bf16[512,1024]{1,0:T(8,128)(2,1)} custom-call(bf16[128,128]{1,0:T(8,128)(2,1)} %get-tuple-element.16.emb_ref), custom_call_target="tpu_custom_call" | custom-call | tf_op jit(solution)/shard_map/talk0/pallas_call | solution.py:258
  22.6 1.5 fusion.8
  24.1 1.5 fusion.10
  25.7 0.1 dynamic-slice_bitcast_fusion.1
  25.8 0.7 copy.14.inv_ref
  26.5 11.6 %multiply_convert_fusion.3 = (bf16[512,4096]{1,0:T(8,128)(2,1)S(1)}, f32[512,4096]{1,0:T(8,128)}) fusion(bf16[512,1024]{1,0:T(8,128)(2,1)S(1)} %fusion.10, bf16[1024,4096]{1,0:T(8,128)(2,1)} %param.14), kind=kOutput, calls=%fused_computation.10 | convolution fusion | flops 4313841664 | bytes 22020096 | tf_op jit(solution)/shard_map/dot_general | solution.py:309
  38.2 2.0 copy-done.1
  40.2 5.4 %convolution_convert_fusion.2.partial_ref = bf16[128,1024]{1,0:T(8,128)(2,1)} fusion(bf16[4096,1024]{1,0:T(8,128)(2,1)} %param.15, bf16[512,4096]{1,0:T(8,128)(2,1)S(1)} %get-tuple-element.17, s32[]{:T(128)S(6)} %select_n.7), kind=kOutput, calls=%fused_computation.32 | convolution fusion | flops 1073872896 | bytes 9699332 | tf_op jit(solution)/shard_map/dot_general | solution.py:313
  45.5 25.7 %talk1.1 = (bf16[512,1024]{1,0:T(8,128)(2,1)}, f32[128,128]{1,0:T(8,128)}) custom-call(bf16[128,1024]{1,0:T(8,128)(2,1)} %convolution_convert_fusion.2.partial_ref, bf16[128,128]{1,0:T(8,128)(2,1)} %tokens_ref.5, f32[128,128]{1,0:T(8,128)} %get-tuple-element.15.perturb_ref, f32[128,128]{1,0:T(8,128)} %target_ref.3), custom_call_target="tpu_custom_call" | custom-call | tf_op jit(solution)/shard_map/talk1/pallas_call | solution.py:258
  71.2 0.0 copy-start.2
  71.2 12.3 %multiply_convert_fusion.2 = bf16[512,4096]{1,0:T(8,128)(2,1)S(1)} fusion(f32[512,4096]{1,0:T(8,128)} %get-tuple-element.18, bf16[512,1024]{1,0:T(8,128)(2,1)} %get-tuple-element.10, bf16[4096,1024]{1,0:T(8,128)(2,1)} %param.15), kind=kOutput, calls=%fused_computation.9 | convolution fusion | flops 4332716032 | bytes 22020096 | tf_op jit(solution)/shard_map/dot_general | solution.py:323
  83.5 0.0 copy-done.2
  83.5 4.2 %fusion.18 = f32[4096,256]{1,0:T(8,128)} fusion(bf16[512,4096]{1,0:T(8,128)(2,1)S(1)} %copy-done.2, bf16[512,1024]{1,0:T(8,128)(2,1)} %get-tuple-element.10, s32[]{:T(128)S(6)} %select_n.6), kind=kOutput, calls=%fused_computation.37 | convolution fusion | flops 1073741824 | bytes 8650756 | tf_op jit(solution)/shard_map/dot_general | solution.py:348
  87.7 7.0 %convolution_convert_fusion.1.partial_ref = bf16[128,1024]{1,0:T(8,128)(2,1)} fusion(bf16[1024,4096]{1,0:T(8,128)(2,1)} %param.14, bf16[512,4096]{1,0:T(8,128)(2,1)S(1)} %multiply_convert_fusion.2, s32[]{:T(128)S(6)} %select_n.7), kind=kOutput, calls=%fused_computation.31 | convolution fusion | flops 1073872896 | bytes 9699332 | tf_op jit(solution)/shard_map/dot_general | solution.py:327
  94.7 3.3 %fusion.21 = f32[256,4096]{1,0:T(8,128)} fusion(bf16[512,4096]{1,0:T(8,128)(2,1)S(1)} %multiply_convert_fusion.2, bf16[512,1024]{1,0:T(8,128)(2,1)S(1)} %fusion.10, s32[]{:T(128)S(6)} %select_n.6), kind=kOutput, calls=%fused_computation.40 | convolution fusion | flops 1073741824 | bytes 8650756 | tf_op jit(solution)/shard_map/dot_general | solution.py:347
  98.1 31.7 %talk2.1 = (bf16[512,1024]{1,0:T(8,128)(2,1)}, f32[128,128]{1,0:T(8,128)}) custom-call(bf16[128,1024]{1,0:T(8,128)(2,1)} %convolution_convert_fusion.1.partial_ref, bf16[128,128]{1,0:T(8,128)(2,1)} %tokens_ref.5, f32[128,128]{1,0:T(8,128)} %get-tuple-element.15.perturb_ref, f32[128,128]{1,0:T(8,128)} %get-tuple-element.11.out_grad_ref, ...), custom_call_target="tpu_custom_call" | custom-call | tf_op jit(solution)/shard_map/talk2/pallas_call | solution.py:258
  129.8 1.5 fusion.11
  131.3 0.0 copy-done.4
  131.3 0.0 slice-start
  131.3 1.7 fusion.13
  133.0 0.0 slice-start.1
  133.0 11.8 %multiply_convert_fusion.1 = (bf16[512,4096]{1,0:T(8,128)(2,1)S(1)}, f32[512,4096]{1,0:T(8,128)}) fusion(bf16[512,1024]{1,0:T(8,128)(2,1)S(1)} %fusion.13, bf16[1024,4096]{1,0:T(8,128)(2,1)} %param.14), kind=kOutput, calls=%fused_computation.7 | convolution fusion | flops 4313841664 | bytes 22020096 | tf_op jit(solution)/shard_map/dot_general | solution.py:309
  144.9 1.9 copy-done
  146.8 0.0 slice-done
  146.8 0.0 slice-done.1
  146.8 2.0 convolution_convert_fusion.partial_ref
  148.8 25.2 %talk3.1 = (bf16[512,1024]{1,0:T(8,128)(2,1)}, f32[128,128]{1,0:T(8,128)}) custom-call(bf16[128,1024]{1,0:T(8,128)(2,1)} %convolution_convert_fusion.partial_ref, bf16[128,128]{1,0:T(8,128)(2,1)} %tokens_ref.5, f32[128,128]{1,0:T(8,128)} %get-tuple-element.34.perturb_ref, f32[128,128]{1,0:T(8,128)} %target_ref.3), custom_call_target="tpu_custom_call" | custom-call | tf_op jit(solution)/shard_map/talk3/pallas_call | solution.py:258
  174.0 19.5 %subtract_convert_fusion.1 = (bf16[256,4096]{1,0:T(8,128)(2,1)}, f32[256,4096]{1,0:T(8,128)}) fusion(bf16[1024,4096]{1,0:T(8,128)(2,1)} %param.14, s32[]{:T(128)S(6)} %select_n.6, f32[256,4096]{1,0:T(8,128)} %fusion.21, f32[512,4096]{1,0:T(8,128)} %get-tuple-element.20, bf16[512,1024]{1,0:T(8,128)(2,1)} %get-tuple-element.14, ...), kind=kOutput, calls=%fused_computation.19 | convolution fusion | flops 5414846464 | bytes 34866176 | tf_op jit(solution)/shard_map/dot_general | solution.py:347
  193.5 9.8 %subtract_convert_fusion = (bf16[4096,256]{1,0:T(8,128)(2,1)}, f32[4096,256]{1,0:T(8,128)}) fusion(bf16[4096,1024]{1,0:T(8,128)(2,1)} %param.15, s32[]{:T(128)S(6)} %select_n.6, f32[4096,256]{1,0:T(8,128)} %fusion.18, bf16[512,4096]{1,0:T(8,128)(2,1)} %copy-done, bf16[512,1024]{1,0:T(8,128)(2,1)} %get-tuple-element.14, f32[4096,256]{1,0:T(8,128)} %param.17), kind=kOutput, calls=%fused_computation.18 | convolution fusion | flops 1082130432 | bytes 21234688 | tf_op jit(solution)/shard_map/dot_general | solution.py:348
  203.3 0.6 copy.16
  (8 shorter events, 0.0 us)
Async XLA Ops:
  38.2 2.0 copy-start.1
  71.2 12.3 %copy-start.2 = (bf16[512,4096]{1,0:T(8,128)(2,1)S(1)}, bf16[512,4096]{1,0:T(8,128)(2,1)}, u32[]{:S(2)}) copy-start(bf16[512,4096]{1,0:T(8,128)(2,1)} %copy-done.1) | copy-start | bytes 12582916
  94.7 36.6 %copy-start.4 = (f32[1024]{0:T(1024)S(1)}, f32[1024]{0:T(1024)}, u32[]{:S(2)}) copy-start(f32[1024]{0:T(1024)} %param.13) | copy-start | bytes 12292
  131.3 15.5 %slice-start = ((s8[8388608]{0:T(1024)(128)(4,1)}), s8[4194304]{0:T(1024)(128)(4,1)S(1)}, s32[]{:S(2)}) async-start(s8[8388608]{0:T(1024)(128)(4,1)} %bitcast.19), calls=%async_computation | async-start | bytes 8388608
  133.0 13.8 %slice-start.1 = ((s8[8388608]{0:T(1024)(128)(4,1)}), s8[4194304]{0:T(1024)(128)(4,1)S(1)}, s32[]{:S(2)}) async-start(s8[8388608]{0:T(1024)(128)(4,1)} %bitcast.19), calls=%async_computation.1 | async-start | bytes 8388608
  144.9 1.9 copy-start
  193.5 9.8 %copy-start.3 = (f32[128,128]{1,0:T(8,128)S(1)}, f32[128,128]{1,0:T(8,128)}, u32[]{:S(2)}) copy-start(f32[128,128]{1,0:T(8,128)} %get-tuple-element.34.perturb_ref) | copy-start | bytes 196612

commit v2 on v1

--- a/solution.py
+++ b/solution.py
@@ -21,7 +21,7 @@
     tangent = jnp.tanh(coeff * (values + 0.044715 * square * values))
     half = 0.5 * (1.0 + tangent)
     slope = half + 0.5 * values * (1.0 - tangent * tangent) * coeff * (1.0 + 3.0 * 0.044715 * square)
-    return values * half, slope
+    return values * half, slope.astype(jnp.bfloat16)
 
 
 class Place:

time: 204 us -> 204 us (level)
  no operation moved by 1% of the time
where the time goes in v2:
time: 204 us
  Pallas kernels  102 us (50%)
  matrix products  86.9 us (43%)
  other arithmetic  7.72 us (4%)
  local copies, waits for them, and re-layouts  6.69 us (3%)
    pallas_call x4, Pallas kernels, talk(): pl.pallas_call(kernel, name=f'talk{number}', out_shape=out_shape, in_spec...  102 us
    dot_general x2, matrix products, shards(): preact = jnp.dot(normed, weight_in, preferred_element_type=jnp.float32)  23.5 us
    dot_general x2, matrix products, shards(): jnp.dot(normed_cols.T, hidden_grad, preferred_element_type=jnp.float32)  22.8 us
    dot_general x2, matrix products, shards(): jnp.dot(hidden.T, grad_cols, preferred_element_type=jnp.float32)  14 us
    dot_general x1, matrix products, shards(): jnp.dot(grad_whole, weight_out.T, preferred_element_type=jnp.float32)  12.3 us
    dot_general x2, matrix products, shards(): jnp.dot(hidden_own, weight_out, preferred_element_type=jnp.float32)  7.37 us
    dot_general x1, matrix products, shards(): jnp.dot(hidden_grad_own, weight_in.T, preferred_element_type=jnp.float32)  6.99 us
    unnamed x15, local copies, waits for them, and re-layouts  4.59 us

profile of v2, /device:TPU:1, one launch (start us, length us, event | category | flops | bytes accessed | tf_op | source)
XLA Modules:
  0.0 203.9 jit_solution(17758883324777232945)
XLA Ops:
  0.6 1.3 dynamic-slice_bitcast_fusion.gain_ref
  1.9 1.5 broadcast_multiply_fusion
  3.4 19.2 %talk0.1 = bf16[512,1024]{1,0:T(8,128)(2,1)} custom-call(bf16[128,128]{1,0:T(8,128)(2,1)} %get-tuple-element.16.emb_ref), custom_call_target="tpu_custom_call" | custom-call | tf_op jit(solution)/shard_map/talk0/pallas_call | solution.py:258
  22.6 1.5 fusion.8
  24.1 1.5 fusion.10
  25.7 0.1 dynamic-slice_bitcast_fusion.1
  25.8 0.7 copy.14.inv_ref
  26.5 11.6 %multiply_convert_fusion.3 = (bf16[512,4096]{1,0:T(8,128)(2,1)S(1)}, f32[512,4096]{1,0:T(8,128)}) fusion(bf16[512,1024]{1,0:T(8,128)(2,1)S(1)} %fusion.10, bf16[1024,4096]{1,0:T(8,128)(2,1)} %param.14), kind=kOutput, calls=%fused_computation.12 | convolution fusion | flops 4313841664 | bytes 22020096 | tf_op jit(solution)/shard_map/dot_general | solution.py:309
  38.2 2.0 copy-done.1
  40.2 5.4 %convolution_convert_fusion.2.partial_ref = bf16[128,1024]{1,0:T(8,128)(2,1)} fusion(bf16[4096,1024]{1,0:T(8,128)(2,1)} %param.15, bf16[512,4096]{1,0:T(8,128)(2,1)S(1)} %get-tuple-element.17, s32[]{:T(128)S(6)} %select_n.7), kind=kOutput, calls=%fused_computation.34 | convolution fusion | flops 1073872896 | bytes 9699332 | tf_op jit(solution)/shard_map/dot_general | solution.py:313
  45.5 25.7 %talk1.1 = (bf16[512,1024]{1,0:T(8,128)(2,1)}, f32[128,128]{1,0:T(8,128)}) custom-call(bf16[128,1024]{1,0:T(8,128)(2,1)} %convolution_convert_fusion.2.partial_ref, bf16[128,128]{1,0:T(8,128)(2,1)} %tokens_ref.5, f32[128,128]{1,0:T(8,128)} %get-tuple-element.15.perturb_ref, f32[128,128]{1,0:T(8,128)} %target_ref.3), custom_call_target="tpu_custom_call" | custom-call | tf_op jit(solution)/shard_map/talk1/pallas_call | solution.py:258
  71.2 0.0 copy-start.2
  71.2 12.3 %multiply_convert_fusion.2 = bf16[512,4096]{1,0:T(8,128)(2,1)S(1)} fusion(bf16[512,1024]{1,0:T(8,128)(2,1)} %get-tuple-element.10, bf16[4096,1024]{1,0:T(8,128)(2,1)} %param.15, f32[512,4096]{1,0:T(8,128)} %get-tuple-element.18), kind=kOutput, calls=%fused_computation.10 | convolution fusion | flops 4336910336 | bytes 22020096 | tf_op jit(solution)/shard_map/dot_general | solution.py:323
  83.5 0.0 copy-done.2
  83.5 4.2 %fusion.18 = f32[4096,256]{1,0:T(8,128)} fusion(bf16[512,4096]{1,0:T(8,128)(2,1)S(1)} %copy-done.2, bf16[512,1024]{1,0:T(8,128)(2,1)} %get-tuple-element.10, s32[]{:T(128)S(6)} %select_n.6), kind=kOutput, calls=%fused_computation.39 | convolution fusion | flops 1073741824 | bytes 8650756 | tf_op jit(solution)/shard_map/dot_general | solution.py:348
  87.7 7.0 %convolution_convert_fusion.1.partial_ref = bf16[128,1024]{1,0:T(8,128)(2,1)} fusion(bf16[1024,4096]{1,0:T(8,128)(2,1)} %param.14, bf16[512,4096]{1,0:T(8,128)(2,1)S(1)} %multiply_convert_fusion.2, s32[]{:T(128)S(6)} %select_n.7), kind=kOutput, calls=%fused_computation.33 | convolution fusion | flops 1073872896 | bytes 9699332 | tf_op jit(solution)/shard_map/dot_general | solution.py:327
  94.7 3.3 %fusion.21 = f32[256,4096]{1,0:T(8,128)} fusion(bf16[512,4096]{1,0:T(8,128)(2,1)S(1)} %multiply_convert_fusion.2, bf16[512,1024]{1,0:T(8,128)(2,1)S(1)} %fusion.10, s32[]{:T(128)S(6)} %select_n.6), kind=kOutput, calls=%fused_computation.42 | convolution fusion | flops 1073741824 | bytes 8650756 | tf_op jit(solution)/shard_map/dot_general | solution.py:347
  98.1 31.7 %talk2.1 = (bf16[512,1024]{1,0:T(8,128)(2,1)}, f32[128,128]{1,0:T(8,128)}) custom-call(bf16[128,1024]{1,0:T(8,128)(2,1)} %convolution_convert_fusion.1.partial_ref, bf16[128,128]{1,0:T(8,128)(2,1)} %tokens_ref.5, f32[128,128]{1,0:T(8,128)} %get-tuple-element.15.perturb_ref, f32[128,128]{1,0:T(8,128)} %get-tuple-element.11.out_grad_ref, ...), custom_call_target="tpu_custom_call" | custom-call | tf_op jit(solution)/shard_map/talk2/pallas_call | solution.py:258
  129.8 1.5 fusion.11
  131.3 0.0 copy-done.4
  131.3 0.0 slice-start
  131.3 1.7 fusion.13
  133.0 0.0 slice-start.1
  133.0 11.8 %multiply_convert_fusion.1 = (bf16[512,4096]{1,0:T(8,128)(2,1)S(1)}, f32[512,4096]{1,0:T(8,128)}) fusion(bf16[512,1024]{1,0:T(8,128)(2,1)S(1)} %fusion.13, bf16[1024,4096]{1,0:T(8,128)(2,1)} %param.14), kind=kOutput, calls=%fused_computation.8 | convolution fusion | flops 4313841664 | bytes 22020096 | tf_op jit(solution)/shard_map/dot_general | solution.py:309
  144.9 1.9 copy-done
  146.8 0.0 slice-done
  146.8 0.0 slice-done.1
  146.8 2.0 convolution_convert_fusion.partial_ref
  148.8 25.2 %talk3.1 = (bf16[512,1024]{1,0:T(8,128)(2,1)}, f32[128,128]{1,0:T(8,128)}) custom-call(bf16[128,1024]{1,0:T(8,128)(2,1)} %convolution_convert_fusion.partial_ref, bf16[128,128]{1,0:T(8,128)(2,1)} %tokens_ref.5, f32[128,128]{1,0:T(8,128)} %get-tuple-element.34.perturb_ref, f32[128,128]{1,0:T(8,128)} %target_ref.3), custom_call_target="tpu_custom_call" | custom-call | tf_op jit(solution)/shard_map/talk3/pallas_call | solution.py:258
  174.0 19.5 %subtract_convert_fusion.1 = (bf16[256,4096]{1,0:T(8,128)(2,1)}, f32[256,4096]{1,0:T(8,128)}) fusion(bf16[1024,4096]{1,0:T(8,128)(2,1)} %param.14, s32[]{:T(128)S(6)} %select_n.6, f32[256,4096]{1,0:T(8,128)} %fusion.21, bf16[512,1024]{1,0:T(8,128)(2,1)} %get-tuple-element.14, bf16[4096,1024]{1,0:T(8,128)(2,1)} %param.15, ...), kind=kOutput, calls=%fused_computation.21 | convolution fusion | flops 5419040768 | bytes 34866176 | tf_op jit(solution)/shard_map/dot_general | solution.py:347
  193.5 9.8 %subtract_convert_fusion = (bf16[4096,256]{1,0:T(8,128)(2,1)}, f32[4096,256]{1,0:T(8,128)}) fusion(bf16[4096,1024]{1,0:T(8,128)(2,1)} %param.15, s32[]{:T(128)S(6)} %select_n.6, f32[4096,256]{1,0:T(8,128)} %fusion.18, bf16[512,4096]{1,0:T(8,128)(2,1)} %copy-done, bf16[512,1024]{1,0:T(8,128)(2,1)} %get-tuple-element.14, f32[4096,256]{1,0:T(8,128)} %param.17), kind=kOutput, calls=%fused_computation.20 | convolution fusion | flops 1082130432 | bytes 21234688 | tf_op jit(solution)/shard_map/dot_general | solution.py:348
  203.3 0.6 copy.16
  (8 shorter events, 0.0 us)
Async XLA Ops:
  38.2 2.0 copy-start.1
  71.2 12.3 %copy-start.2 = (bf16[512,4096]{1,0:T(8,128)(2,1)S(1)}, bf16[512,4096]{1,0:T(8,128)(2,1)}, u32[]{:S(2)}) copy-start(bf16[512,4096]{1,0:T(8,128)(2,1)} %copy-done.1) | copy-start | bytes 12582916
  94.7 36.6 %copy-start.4 = (f32[1024]{0:T(1024)S(1)}, f32[1024]{0:T(1024)}, u32[]{:S(2)}) copy-start(f32[1024]{0:T(1024)} %param.13) | copy-start | bytes 12292
  131.3 15.5 %slice-start = ((s8[8388608]{0:T(1024)(128)(4,1)}), s8[4194304]{0:T(1024)(128)(4,1)S(1)}, s32[]{:S(2)}) async-start(s8[8388608]{0:T(1024)(128)(4,1)} %bitcast.19), calls=%async_computation | async-start | bytes 8388608
  133.0 13.8 %slice-start.1 = ((s8[8388608]{0:T(1024)(128)(4,1)}), s8[4194304]{0:T(1024)(128)(4,1)S(1)}, s32[]{:S(2)}) async-start(s8[8388608]{0:T(1024)(128)(4,1)} %bitcast.19), calls=%async_computation.1 | async-start | bytes 8388608
  144.9 1.9 copy-start
  193.5 9.8 %copy-start.3 = (f32[128,128]{1,0:T(8,128)S(1)}, f32[128,128]{1,0:T(8,128)}, u32[]{:S(2)}) copy-start(f32[128,128]{1,0:T(8,128)} %get-tuple-element.34.perturb_ref) | copy-start | bytes 196612
